TPU v7x, 256 devices: a 2x2x32 block of a 4x8x32 slice. The times are simulated.
256 devices in a mesh: cuts: 4 (over y, x), wide: 32 (over z), batch: 2 (over core).
Axes of the slice: x: 2, y: 2, z: 32, core: 2. Of those that a mesh axis runs over, the one named last changes fastest.
The devices are a block of a 4x8x32 slice.
Arguments:
- initial: bfloat16 [2, 128, 2, 2, 256, 256], P('batch', 'cuts', None, None, None, 'wide'), parts along dimension 1, may hold values from -6 to 6
- branches: bfloat16 [8, 2, 2, 256, 2, 256], P(None, None, None, 'batch'), may hold values from -0.1875 to 0.1875
- projectors: float32 [8, 2, 2, 2], replicated, may hold values from -4 to 4
- bits: int32 [2, 8], P('batch'), may hold values from 0 to 1
Outputs:
- amplitudes: float32 [2, 128, 2, 2, 256, 256], P('batch', 'cuts', None, None, 'wide'), parts along dimension 1
There are 4 independent parts, one for each index of `cuts`. A program takes and returns all parts, laid end to end along the dimension named above; an argument that names none is the same for every part. Nothing has to cross between parts.
Inputs may be any that keep to these rules, and one draw needn't show every extreme that they name: `bits`: each entry is a bit.
All inputs are finite; a program needn't handle non-finite values.
Results may differ from a plain program's by a relative error of at most 0.014.
Values may be sent and summed in bfloat16 or wider, within the bound.
A program may use at most 64 MiB of HBM per device.

v0:
```python
import jax
import jax.numpy as jnp
from jax import lax
from jax.sharding import PartitionSpec as P


def copy_for_each(value, axis):
    copies = jnp.broadcast_to(value, (lax.axis_size(axis), *value.shape))
    return lax.all_to_all(copies, axis, split_axis=0, concat_axis=0, tiled=True)


def laid_out(pieces, dim):
    pieces = jnp.moveaxis(pieces, 0, dim)
    lengths = pieces.shape
    return pieces.reshape(*lengths[:dim], lengths[dim] * lengths[dim + 1], *lengths[dim + 2 :])


def gathered_copies(value, axis, dim):
    pieces = copy_for_each(value, axis)
    return laid_out(pieces, dim)


def contract(state, branch, select):
    prod = jnp.einsum("ncphuv,thugw->ncptgvw", state, branch, preferred_element_type=jnp.float32)
    real_part = prod[:, :, 0, 0] - prod[:, :, 1, 1]
    imag_part = prod[:, :, 0, 1] + prod[:, :, 1, 0]
    proj_re = select[:, 0][:, None, :, None, None]
    proj_im = select[:, 1][:, None, :, None, None]
    out_re = proj_re * real_part - proj_im * imag_part
    out_im = proj_re * imag_part + proj_im * real_part
    return jnp.stack([out_re, out_im], axis=2)


def advance(block, branch, select, final):
    result = contract(block, branch, select)
    if final:
        return result
    return result.astype(jnp.bfloat16)


def branch_of(branches, step):
    return gathered_copies(branches[step], "batch", 2)


def select_of(projectors, bits, step):
    chosen = (bits[:, step] == 1)[:, None, None]
    return jnp.where(chosen, projectors[step, 1][None], projectors[step, 0][None])


def shards(initial, branches, projectors, bits):
    steps_total = branches.shape[0]
    state = lax.all_to_all(initial, "wide", split_axis=1, concat_axis=5, tiled=True)
    for step in range(steps_total):
        branch = branch_of(branches, step)
        select = select_of(projectors, bits, step)
        state = advance(state, branch, select, step == steps_total - 1)
    return lax.all_to_all(state, "wide", split_axis=4, concat_axis=1, tiled=True)


def solution(mesh):
    in_specs = (
        P("batch", "cuts", None, None, None, "wide"),
        P(None, None, None, "batch", None, None),
        P(),
        P("batch", None),
    )
    out_specs = P("batch", "cuts", None, None, "wide", None)
    return jax.shard_map(shards, mesh=mesh, in_specs=in_specs, out_specs=out_specs, check_vma=False)
```

profile of v0, /device:TPU:37, one launch (start us, length us, event | category | flops | bytes accessed | tf_op | source)
XLA Modules:
  0.0 275.5 jit_solution(9295105258477170813)
XLA Ops:
  0.0 6.0 %slice_bitcast_fusion.9 = (bf16[2,2,128,2,256]{4,3,2,1,0:T(2,128)(2,1)S(1)}, bf16[2,2,128,2,256]{4,3,2,1,0:T(2,128)(2,1)}, bf16[2,2,128,2,256]{4,3,2,1,0:T(2,128...) fusion(bf16[8,2,2,128,2,256]{5,4,3,2,1,0:T(2,128)(2,1)} %param.5), kind=kLoop, calls=%fused_computation.91 | loop fusion | bytes 8388608 | tf_op jit(solution)/shard_map/squeeze | solution.py:42
  6.4 1.2 broadcast_in_dim.107
  7.6 24.0 %all-to-all-start = ((bf16[2,2,2,128,2,256]{3,5,2,4,1,0:T(8,128)(2,1)}), bf16[2,2,2,128,2,256]{3,5,2,4,1,0:T(8,128)(2,1)S(1)}, u32[]{:S(2)}, u32[]{:S(2)}) async-start(bf16[2,2,2,128,2,256]{3,5,2,4,1,0:T(8,128)(2,1)} %broadcast_in_dim.107), calls=%async_computation | async-start | bytes 2097152 | tf_op jit(solution)/shard_map/all_to_all | solution.py:9
  36.5 1.1 broadcast_in_dim.108
  37.7 5.1 %all_to_all.73 = bf16[2,2,2,128,2,256]{5,3,2,4,1,0:T(8,128)(2,1)} all-to-all(bf16[2,2,2,128,2,256]{5,3,2,4,1,0:T(8,128)(2,1)S(1)} %broadcast_in_dim.108), channel_id=1, replica_groups=mesh['cuts'=4,'wide'=32,'batch'=2] {'batch'}, dimensions={0} | all-to-all | bytes 2097152 | tf_op jit(solution)/shard_map/all_to_all | solution.py:9
  42.8 4.6 %all_to_all.74 = bf16[2,2,2,128,2,256]{5,3,2,4,1,0:T(8,128)(2,1)S(1)} all-to-all(bf16[2,2,2,128,2,256]{5,3,2,4,1,0:T(8,128)(2,1)S(1)} %broadcast_in_dim.109), channel_id=1, replica_groups=mesh['cuts'=4,'wide'=32,'batch'=2] {'batch'}, dimensions={0} | all-to-all | bytes 2097152 | tf_op jit(solution)/shard_map/all_to_all | solution.py:9
  47.5 4.7 %all_to_all.75 = bf16[2,2,2,128,2,256]{5,3,2,4,1,0:T(8,128)(2,1)S(1)} all-to-all(bf16[2,2,2,128,2,256]{5,3,2,4,1,0:T(8,128)(2,1)S(1)} %broadcast_in_dim.110), channel_id=1, replica_groups=mesh['cuts'=4,'wide'=32,'batch'=2] {'batch'}, dimensions={0} | all-to-all | bytes 2097152 | tf_op jit(solution)/shard_map/all_to_all | solution.py:9
  52.4 5.5 %all_to_all.76 = bf16[2,2,2,128,2,256]{5,3,2,4,1,0:T(8,128)(2,1)} all-to-all(bf16[2,2,2,128,2,256]{5,3,2,4,1,0:T(8,128)(2,1)S(1)} %broadcast_in_dim.111), channel_id=1, replica_groups=mesh['cuts'=4,'wide'=32,'batch'=2] {'batch'}, dimensions={0} | all-to-all | bytes 2097152 | tf_op jit(solution)/shard_map/all_to_all | solution.py:9
  58.0 5.5 %all_to_all.77 = bf16[2,2,2,128,2,256]{5,3,2,4,1,0:T(8,128)(2,1)} all-to-all(bf16[2,2,2,128,2,256]{5,3,2,4,1,0:T(8,128)(2,1)S(1)} %broadcast_in_dim.112), channel_id=1, replica_groups=mesh['cuts'=4,'wide'=32,'batch'=2] {'batch'}, dimensions={0} | all-to-all | bytes 2097152 | tf_op jit(solution)/shard_map/all_to_all | solution.py:9
  63.7 5.5 %all_to_all.78 = bf16[2,2,2,128,2,256]{5,3,2,4,1,0:T(8,128)(2,1)} all-to-all(bf16[2,2,2,128,2,256]{5,3,2,4,1,0:T(8,128)(2,1)S(1)} %broadcast_in_dim.113), channel_id=1, replica_groups=mesh['cuts'=4,'wide'=32,'batch'=2] {'batch'}, dimensions={0} | all-to-all | bytes 2097152 | tf_op jit(solution)/shard_map/all_to_all | solution.py:9
  69.3 5.4 %all_to_all.79 = bf16[2,2,2,128,2,256]{5,3,2,4,1,0:T(8,128)(2,1)} all-to-all(bf16[2,2,2,128,2,256]{5,3,2,4,1,0:T(8,128)(2,1)S(1)} %broadcast_in_dim.114), channel_id=1, replica_groups=mesh['cuts'=4,'wide'=32,'batch'=2] {'batch'}, dimensions={0} | all-to-all | bytes 2097152 | tf_op jit(solution)/shard_map/all_to_all | solution.py:9
  74.7 13.7 %all-to-all-start.1 = ((bf16[1,32,2,2,256,8]{4,5,3,2,0,1:T(8,128)(2,1)}), bf16[1,32,2,2,256,8]{4,5,3,2,0,1:T(8,128)(2,1)}, u32[]{:S(2)}, u32[]{:S(2)}) async-start(bf16[1,32,2,2,256,8]{4,5,3,2,0,1:T(8,128)(2,1)} %bitcast.356), calls=%async_computation.1 | async-start | bytes 1048576 | tf_op jit(solution)/shard_map/all_to_all | solution.py:52
  92.8 2.0 copy.43
  94.9 2.6 reshape.1163
  97.5 1.0 copy.50
  99.8 1.1 copy.52
  100.9 1.1 copy.55
  102.0 1.0 copy.58
  104.9 47.1 %all-to-all-done.1 = bf16[1,32,2,2,256,8]{4,5,3,2,0,1:T(8,128)(2,1)} async-done(((bf16[1,32,2,2,256,8]{4,5,3,2,0,1:T(8,128)(2,1)}), bf16[1,32,2,2,256,8]{4,5,3,2,0,1:T(8,128)(2,1)}, u32[]{:S(2)}, u32[]{:S(2)}) %all-to-all-start.1) | async-done | bytes 524320 | tf_op jit(solution)/shard_map/all_to_all | solution.py:52
  152.0 2.1 convolution_bitcast_fusion.7
  154.4 1.0 copy-done.3
  158.3 1.0 copy-done.1
  166.0 108.3 %all_to_all.80 = f32[1,1,2,2,256,256]{5,3,2,1,0,4:T(2,128)S(1)} all-to-all(f32[1,1,2,2,256,256]{5,3,2,1,0,4:T(2,128)S(1)} %copy.69), channel_id=1, replica_groups=mesh['cuts'=4,'wide'=32,'batch'=2] {'wide'}, dimensions={4} | all-to-all | bytes 2097152 | tf_op jit(solution)/shard_map/all_to_all | solution.py:57
  274.3 1.2 copy.108
  (80 shorter events, 18.2 us)
Async XLA Ops:
  7.6 28.9 %all-to-all-start = ((bf16[2,2,2,128,2,256]{3,5,2,4,1,0:T(8,128)(2,1)}), bf16[2,2,2,128,2,256]{3,5,2,4,1,0:T(8,128)(2,1)S(1)}, u32[]{:S(2)}, u32[]{:S(2)}) async-start(bf16[2,2,2,128,2,256]{3,5,2,4,1,0:T(8,128)(2,1)} %broadcast_in_dim.107), calls=%async_computation | async-start | bytes 2097152 | tf_op jit(solution)/shard_map/all_to_all | solution.py:9
  31.6 1.2 copy-start.15
  31.6 1.4 copy-start.14
  31.6 2.3 copy-start.13
  47.4 4.8 %copy-start.12 = (bf16[2,2,128,2,256]{4,2,1,3,0:T(8,128)(2,1)S(1)}, bf16[2,2,128,2,256]{4,2,1,3,0:T(8,128)(2,1)}, u32[]{:S(2)}) copy-start(bf16[2,2,128,2,256]{4,2,1,3,0:T(8,128)(2,1)} %copy.57) | copy-start | bytes 1572868
  52.3 5.6 %copy-start.11 = (bf16[2,2,128,2,256]{4,2,1,3,0:T(8,128)(2,1)S(1)}, bf16[2,2,128,2,256]{4,2,1,3,0:T(8,128)(2,1)}, u32[]{:S(2)}) copy-start(bf16[2,2,128,2,256]{4,2,1,3,0:T(8,128)(2,1)} %copy.60) | copy-start | bytes 1572868
  57.9 5.7 %copy-start.10 = (bf16[2,2,128,2,256]{4,2,1,3,0:T(8,128)(2,1)S(1)}, bf16[2,2,128,2,256]{4,2,1,3,0:T(8,128)(2,1)}, u32[]{:S(2)}) copy-start(bf16[2,2,128,2,256]{4,2,1,3,0:T(8,128)(2,1)} %copy.63) | copy-start | bytes 1572868
  63.6 5.6 %copy-start.9 = (bf16[2,2,128,2,256]{4,2,1,3,0:T(8,128)(2,1)S(1)}, bf16[2,2,128,2,256]{4,2,1,3,0:T(8,128)(2,1)}, u32[]{:S(2)}) copy-start(bf16[2,2,128,2,256]{4,2,1,3,0:T(8,128)(2,1)} %copy.66) | copy-start | bytes 1572868
  69.2 19.2 %copy-start.17 = (s32[1,8]{1,0:T(1,128)S(1)}, s32[1,8]{1,0:T(1,128)}, u32[]{:S(2)}) copy-start(s32[1,8]{1,0:T(1,128)} %param.7) | copy-start | bytes 100
  74.7 77.3 %all-to-all-start.1 = ((bf16[1,32,2,2,256,8]{4,5,3,2,0,1:T(8,128)(2,1)}), bf16[1,32,2,2,256,8]{4,5,3,2,0,1:T(8,128)(2,1)}, u32[]{:S(2)}, u32[]{:S(2)}) async-start(bf16[1,32,2,2,256,8]{4,5,3,2,0,1:T(8,128)(2,1)} %bitcast.356), calls=%async_computation.1 | async-start | bytes 1048576 | tf_op jit(solution)/shard_map/all_to_all | solution.py:52
  94.9 2.6 copy-start.4
  99.8 2.2 copy-start.5
  100.9 2.1 copy-start.6
  102.0 1.7 copy-start.7
  103.0 1.3 copy-start.8
  103.7 0.8 copy-start.16
  154.1 1.2 copy-start.3
  156.1 1.2 copy-start.2
  158.0 1.2 copy-start.1
  160.0 1.2 copy-start
where the time goes:
time: 281 us; the launch traced here: 275 us
  blocking collectives  145 us (52%)
  waiting for transfers between devices  47.1 us (17%)
  starting transfers between devices  37.7 us (13%)
  local copies, waits for them, and re-layouts  31.1 us (11%)
  matrix products  7.15 us (3%)
  between operations  5.39 us (2%)
    all_to_all x1, blocking collectives, shards(): lax.all_to_all(state, 'wide', split_axis=4, concat_axis=1, tiled=True)  108 us
    all_to_all x1, waiting for transfers between devices, shards(): lax.all_to_all(initial, 'wide', split_axis=1, concat_axis=5, tiled=True)  47.1 us
    all_to_all x7, blocking collectives, copy_for_each(): return lax.all_to_all(copies, axis, split_axis=0, concat_axis=0, tiled=True)  36.3 us
    all_to_all x1, starting transfers between devices, copy_for_each(): return lax.all_to_all(copies, axis, split_axis=0, concat_axis=0, tiled=True)  24 us
    all_to_all x1, starting transfers between devices, shards(): lax.all_to_all(initial, 'wide', split_axis=1, concat_axis=5, tiled=True)  13.7 us
    squeeze x9, local copies, waits for them, and re-layouts, branch_of(): return gathered_copies(branches[step], 'batch', 2)  11 us
    dot_general x8, matrix products, contract(): jnp.einsum('ncphuv,thugw->ncptgvw', state, branch, preferred_element_type...  7.15 us
    transpose x8, local copies, waits for them, and re-layouts, laid_out(): pieces = jnp.moveaxis(pieces, 0, dim)  6.56 us
  transfers between devices with their start and end apart: 2, of which 1 were waited for; matrix products, arithmetic and copies ran while one was open for 5% of the time, Pallas kernels for 0%

commit v1 on v0

v1 whole, which is shorter than its diff:
```python
import functools

import jax
import jax.numpy as jnp
from jax import lax
from jax.experimental import pallas as pl
from jax.experimental.pallas import tpu as pltpu
from jax.sharding import PartitionSpec as P

MESH = pl.DeviceIdType.MESH
BF16, F32 = jnp.bfloat16, jnp.float32


def dot(a, b, dims=((1,), (0,))):
    return lax.dot_general(a, b, (dims, ((), ())), preferred_element_type=F32)


def hops_of(n):
    order = [(n // 2, 0), (-(n // 2), 1)]
    for far in range(n // 2 - 1, 0, -1):
        order += [(far, None), (-far, None)]
    return order


def kernel(n, x_hbm, b_hbm, p_hbm, bits_hbm, out, parts, even_w, odd_w, rows_t, rows, send, last, p_s, bits_s,
           send1, recv1, send2, recv2, bsend, brecv, bown, small):
    z = lax.axis_index("wide")
    core = lax.axis_index("batch")
    wide, cols = x_hbm.shape[0] // n, x_hbm.shape[1]
    group = cols // 4
    steps = b_hbm.shape[0]
    hops = hops_of(n)

    barrier = pltpu.get_barrier_semaphore()
    pl.semaphore_signal(barrier, inc=1, device_id={"batch": 1 - core}, device_id_type=MESH)
    for d in range(1, n):
        pl.semaphore_signal(barrier, inc=1, device_id={"wide": lax.rem(z + d, n)}, device_id_type=MESH)
    pl.semaphore_wait(barrier, n)

    def block(ref, index, piece):
        at = pl.ds(pl.multiple_of(index * wide, wide), wide)
        if piece is None:
            return ref.at[at, :]
        return ref.at[at, pl.ds(piece * (cols // 2), cols // 2)]

    def exchange(src, dst, ssem, rsem):
        copies = []
        for i, (d, piece) in enumerate(hops):
            to = lax.rem(z + d + n, n)
            copies.append(pltpu.make_async_remote_copy(
                src_ref=block(src, to, piece), dst_ref=block(dst, z, piece), send_sem=ssem.at[i], recv_sem=rsem.at[i],
                device_id={"wide": to}, device_id_type=MESH))
        return copies

    first = exchange(x_hbm, rows_t, send1, recv1)
    for copy in first:
        copy.start()

    def push(s):
        return pltpu.make_async_remote_copy(
            src_ref=b_hbm.at[s], dst_ref=parts.at[core, s], send_sem=bsend.at[s], recv_sem=brecv.at[s],
            device_id={"batch": 1 - core}, device_id_type=MESH)

    def pull(s):
        return pltpu.make_async_copy(b_hbm.at[s], parts.at[core, s], bown.at[s])

    for s in range(steps):
        push(s).start()
        pull(s).start()
    local = [pltpu.make_async_copy(p_hbm, p_s, small.at[0]), pltpu.make_async_copy(bits_hbm, bits_s, small.at[1]),
             pltpu.make_async_copy(block(x_hbm, z, None), block(rows_t, z, None), small.at[2])]
    for copy in local:
        copy.start()

    depth, lanes = b_hbm.shape[3], b_hbm.shape[4]
    half = group // 2
    quarter = half // 2

    def arrived(s):
        pull(s).wait()
        push(s).wait_recv()

    def pair(h, s, uh, at):
        return jnp.concatenate([parts[uh, s, 0, h, at, :], parts[uh, s, 1, h, at, :]], axis=1)

    def one_hot(shape, hit):
        return jnp.where(hit(lax.broadcasted_iota(jnp.int32, shape, 0), lax.broadcasted_iota(jnp.int32, shape, 1)), 1.0, 0.0).astype(BF16)

    def prepare_even(i, s):
        perm = one_hot((2 * half, 2 * half), lambda j, r: r == (j % quarter) * 4 + j // quarter)
        for h in range(2):
            for uh in range(2):
                for ub in range(2):
                    got = dot(perm, pair(h, s, uh, pl.ds(ub * 4 * quarter, 4 * quarter))).astype(BF16)
                    for wt in range(2):
                        for g in range(2):
                            k = (wt * 2 + g) * quarter
                            re, im = got[k:k + quarter, :lanes], got[k:k + quarter, lanes:]
                            u = uh * half + ub * quarter
                            for p, q, what in ((0, 0, re), (0, 1, im), (1, 0, -im), (1, 1, re)):
                                even_w[i, pl.ds((p * 2 + h) * group + u, quarter), pl.ds((q * 2 + g) * group + wt * lanes, lanes)] = what

    def prepare_odd(i, s):
        perm = one_hot((depth, depth), lambda r, j: r == (j % half) * 4 + j // half)
        for h in range(2):
            for uh in range(2):
                got = dot(pair(h, s, uh, slice(None)), perm, ((0,), (0,))).astype(BF16)
                for wt in range(2):
                    for g in range(2):
                        k = (wt * 2 + g) * half
                        re, im = got[:lanes, k:k + half], got[lanes:, k:k + half]
                        for p, q, what in ((0, 0, re), (0, 1, im), (1, 0, -im), (1, 1, re)):
                            odd_w[i, pl.ds((q * 2 + g) * group + wt * lanes, lanes), pl.ds((p * 2 + h) * group + uh * half, half)] = what

    def prepare(i, _):
        arrived(2 * i)
        prepare_even(i, 2 * i)
        arrived(2 * i + 1)
        prepare_odd(i, 2 * i + 1)
        return 0

    lax.fori_loop(0, 3, prepare, 0)
    arrived(6)
    prepare_odd(3, 6)

    for copy in local:
        copy.wait()

    def project(s, g, y_re, y_im):
        one = bits_s[0, s] == 1
        p_re = jnp.where(one, p_s[1, 0, g, s], p_s[0, 0, g, s])
        p_im = jnp.where(one, p_s[1, 1, g, s], p_s[0, 1, g, s])
        return p_re * y_re - p_im * y_im, p_re * y_im + p_im * y_re

    def at(q, g):
        return pl.ds((q * 2 + g) * group, group)

    for copy in first:
        copy.wait_recv()

    def two_steps(i, _):
        for g in range(2):
            z_re, z_im = project(2 * i, g, dot(rows_t[...], even_w[i, :, at(0, g)]), dot(rows_t[...], even_w[i, :, at(1, g)]))
            rows[at(0, g), :] = z_re.astype(BF16)
            rows[at(1, g), :] = z_im.astype(BF16)
        for g in range(2):
            z_re, z_im = project(2 * i + 1, g, dot(odd_w[i, at(0, g), :], rows[...]), dot(odd_w[i, at(1, g), :], rows[...]))
            rows_t[:, at(0, g)] = z_re.astype(BF16)
            rows_t[:, at(1, g)] = z_im.astype(BF16)
        return 0

    lax.fori_loop(0, 3, two_steps, 0)
    for g in range(2):
        z_re, z_im = project(6, g, dot(odd_w[3, at(0, g), :], rows_t[...], ((1,), (1,))),
                             dot(odd_w[3, at(1, g), :], rows_t[...], ((1,), (1,))))
        send[:, at(0, g)] = z_re.astype(BF16)
        send[:, at(1, g)] = z_im.astype(BF16)

    second = exchange(send, last, send2, recv2)
    for copy in second:
        copy.start()
    own = pltpu.make_async_copy(block(send, z, None), block(last, z, None), small.at[0])
    own.start()
    arrived(7)
    prepare_even(3, 7)
    for s in range(steps):
        push(s).wait_send()
    for copy in first:
        copy.wait_send()
    own.wait()
    for copy in second:
        copy.wait_recv()
    for g in range(2):
        z_re, z_im = project(7, g, dot(last[...], even_w[3, :, at(0, g)]), dot(last[...], even_w[3, :, at(1, g)]))
        out[0, :, 0, g] = z_re.reshape(n, wide, group)
        out[0, :, 1, g] = z_im.reshape(n, wide, group)
    for copy in second:
        copy.wait_send()


def shards(n, initial, branches, projectors, bits):
    _, columns, _, _, group, wide = initial.shape
    steps, _, _, half, _, _ = branches.shape
    x = initial[0].transpose(0, 4, 1, 2, 3).reshape(columns * wide, 4 * group)
    b = branches.reshape(steps, 2, 2, half, 2, 2, group // 2).transpose(0, 1, 2, 3, 5, 4, 6).reshape(steps, 2, 2, half * 4, group // 2)
    hops = len(hops_of(n))
    return pl.pallas_call(
        functools.partial(kernel, n),
        out_shape=jax.ShapeDtypeStruct((1, columns, 2, 2, wide, group), F32),
        in_specs=[pl.BlockSpec(memory_space=pl.ANY)] * 4,
        out_specs=pl.BlockSpec(memory_space=pltpu.VMEM),
        scratch_shapes=[
            pltpu.VMEM((2, steps, 2, 2, half * 4, group // 2), BF16),
            pltpu.VMEM((4, 4 * group, 4 * group), BF16),
            pltpu.VMEM((4, 4 * group, 4 * group), BF16),
            pltpu.VMEM((group, 4 * group), BF16),
            pltpu.VMEM((4 * group, group), BF16),
            pltpu.VMEM((group, 4 * group), BF16),
            pltpu.VMEM((group, 4 * group), BF16),
            pltpu.SMEM((2, 2, 2, steps), F32),
            pltpu.SMEM((1, steps), jnp.int32),
            pltpu.SemaphoreType.DMA((hops,)),
            pltpu.SemaphoreType.DMA((hops,)),
            pltpu.SemaphoreType.DMA((hops,)),
            pltpu.SemaphoreType.DMA((hops,)),
            pltpu.SemaphoreType.DMA((steps,)),
            pltpu.SemaphoreType.DMA((steps,)),
            pltpu.SemaphoreType.DMA((steps,)),
            pltpu.SemaphoreType.DMA((3,)),
        ],
        compiler_params=pltpu.CompilerParams(collective_id=0, has_side_effects=True, vmem_limit_bytes=60 * 2**20),
    )(x, b, projectors.transpose(1, 2, 3, 0), bits)


def solution(mesh):
    in_specs = (
        P("batch", "cuts", None, None, None, "wide"),
        P(None, None, None, "batch", None, None),
        P(),
        P("batch", None),
    )
    out_specs = P("batch", "cuts", None, None, "wide", None)
    return jax.shard_map(functools.partial(shards, mesh.shape["wide"]), mesh=mesh, in_specs=in_specs, out_specs=out_specs, check_vma=False)
```

time: 281 us -> 136 us (0.48); the launches traced: 275 us -> 134 us
  blocking collectives: 145 us -> 0 us
  Pallas kernels: 0 us -> 132 us
  waiting for transfers between devices: 47.1 us -> 0 us
  starting transfers between devices: 37.7 us -> 0 us
  local copies, waits for them, and re-layouts: 31.1 us -> 2.31 us
  matrix products: 7.15 us -> 0 us
  between operations: 5.39 us -> 0.01 us
    all_to_all x8 -> x0, blocking collectives: 145 us -> none  [the longest x1 108 us: shards(): lax.all_to_all(state, 'wide', split_axis=4, concat_axis=1, tiled=True)]
    pallas_call x0 -> x1, Pallas kernels: none -> 132 us  [shards(): pl.pallas_call(functools.partial(kernel, n), out_shape=jax.ShapeDtypeStru...]
    all_to_all x2 -> x0, waiting for transfers between devices: 47.1 us -> none  [the longest x1 47.1 us: shards(): lax.all_to_all(initial, 'wide', split_axis=1, concat_axis=5, tiled=True)]
    all_to_all x2 -> x0, starting transfers between devices: 37.7 us -> none  [the longest x1 24 us: copy_for_each(): return lax.all_to_all(copies, axis, split_axis=0, concat_axis=0, tiled=True)]
    squeeze x9 -> x0, local copies, waits for them, and re-layouts: 11 us -> none  [branch_of(): return gathered_copies(branches[step], 'batch', 2)]
    dot_general x8 -> x0, matrix products: 7.15 us -> none  [contract(): jnp.einsum('ncphuv,thugw->ncptgvw', state, branch, preferred_element_type...]
    transpose x8 -> x0, local copies, waits for them, and re-layouts: 6.56 us -> none  [laid_out(): pieces = jnp.moveaxis(pieces, 0, dim)]
    unnamed x36 -> x1, local copies, waits for them, and re-layouts: 5.39 us -> 2.31 us
  transfers between devices with their start and end apart: 2 -> 0, of which waited for: 1 -> 0; matrix products, arithmetic and copies ran while one was open for 5% -> 0% of each run, Pallas kernels for 0% -> 0%
where the time goes in v1:
time: 136 us; the launch traced here: 134 us
  Pallas kernels  132 us (97%)
  local copies, waits for them, and re-layouts  2.31 us (2%)
    pallas_call x1, Pallas kernels, shards(): pl.pallas_call(functools.partial(kernel, n), out_shape=jax.ShapeDtypeStru...  132 us

profile of v1, /device:TPU:37, one launch (start us, length us, event | category | flops | bytes accessed | tf_op | source)
XLA Modules:
  0.0 134.3 jit_solution(15680926434007490654)
XLA Ops:
  0.0 132.0 %shard_map.46 = f32[1,32,2,2,8,256]{5,4,3,2,1,0:T(8,128)} custom-call(bf16[256,1024]{1,0:T(8,128)(2,1)} %bitcast.12, bf16[8,2,2,512,128]{4,3,2,1,0:T(8,128)(2,1)} %bitcast.11, f32[2,2,2,8]{3,2,1,0:T(2,128)} %bitcast.13, s32[1,8]{1,0:T(1,128)} %bits_hbm.1), custom_call_target="tpu_custom_call" | custom-call | tf_op jit(solution)/shard_map/pallas_call | solution.py:187
  132.0 2.3 %copy.7 = f32[1,32,2,2,8,256]{5,4,3,2,1,0:T(8,128)} copy(f32[1,32,2,2,8,256]{5,4,3,2,1,0:T(8,128)} %shard_map.46) | data formatting | bytes 2097152

commit v2 on v1

--- a/solution.py
+++ b/solution.py
@@ -22,8 +22,19 @@
     return order
 
 
+NEAR = 3
+
+
+def chain_of(n):
+    reach, rounds = min(NEAR, n // 2), []
+    while reach < n // 2:
+        rounds.append(min(reach, n // 2 - reach))
+        reach += rounds[-1]
+    return rounds
+
+
 def kernel(n, x_hbm, b_hbm, p_hbm, bits_hbm, out, parts, even_w, odd_w, rows_t, rows, send, last, p_s, bits_s,
-           send1, recv1, send2, recv2, bsend, brecv, bown, small):
+           send1, recv1, send2, recv2, bsend, brecv, bown, small, chain):
     z = lax.axis_index("wide")
     core = lax.axis_index("batch")
     wide, cols = x_hbm.shape[0] // n, x_hbm.shape[1]
@@ -33,9 +44,10 @@
 
     barrier = pltpu.get_barrier_semaphore()
     pl.semaphore_signal(barrier, inc=1, device_id={"batch": 1 - core}, device_id_type=MESH)
-    for d in range(1, n):
-        pl.semaphore_signal(barrier, inc=1, device_id={"wide": lax.rem(z + d, n)}, device_id_type=MESH)
-    pl.semaphore_wait(barrier, n)
+    for d in range(1, NEAR + 1):
+        for to in (d, n - d):
+            pl.semaphore_signal(barrier, inc=1, device_id={"wide": lax.rem(z + to, n)}, device_id_type=MESH)
+    pl.semaphore_wait(barrier, 2 * NEAR + 1)
 
     def block(ref, index, piece):
         at = pl.ds(pl.multiple_of(index * wide, wide), wide)
@@ -52,10 +64,6 @@
                 device_id={"wide": to}, device_id_type=MESH))
         return copies
 
-    first = exchange(x_hbm, rows_t, send1, recv1)
-    for copy in first:
-        copy.start()
-
     def push(s):
         return pltpu.make_async_remote_copy(
             src_ref=b_hbm.at[s], dst_ref=parts.at[core, s], send_sem=bsend.at[s], recv_sem=brecv.at[s],
@@ -64,9 +72,43 @@
     def pull(s):
         return pltpu.make_async_copy(b_hbm.at[s], parts.at[core, s], bown.at[s])
 
+    first = exchange(x_hbm, rows_t, send1, recv1)
+
+    def start(nearest, farthest):
+        for (d, _), copy in reversed(list(zip(hops, first))):
+            if nearest <= abs(d) <= farthest:
+                copy.start()
+
+    rounds = chain_of(n)
+    reach = NEAR
+    start(1, reach)
     for s in range(steps):
         push(s).start()
         pull(s).start()
+    near = 2 * NEAR
+    for k, hop in enumerate(rounds):
+        pl.semaphore_signal(chain.at[k, 0], inc=1, device_id={"wide": lax.rem(z + hop, n)}, device_id_type=MESH)
+        pl.semaphore_signal(chain.at[k, 1], inc=1, device_id={"wide": lax.rem(z + n - hop, n)}, device_id_type=MESH)
+        pl.semaphore_wait(chain.at[k, 0], 1)
+        pl.semaphore_wait(chain.at[k, 1], 1)
+        if reach < near:
+            start(reach + 1, near)
+        reach += hop
+
+    def rest(odd):
+        for dests in (0, 1):
+            for (d, _), copy in zip(hops, first):
+                if abs(d) > near and (d + odd + dests) % 2 == 0:
+                    copy.start()
+
+    @pl.when(lax.rem(z, 2) == 0)
+    def _():
+        rest(0)
+
+    @pl.when(lax.rem(z, 2) == 1)
+    def _():
+        rest(1)
+
     local = [pltpu.make_async_copy(p_hbm, p_s, small.at[0]), pltpu.make_async_copy(bits_hbm, bits_s, small.at[1]),
              pltpu.make_async_copy(block(x_hbm, z, None), block(rows_t, z, None), small.at[2])]
     for copy in local:
@@ -207,6 +249,7 @@
             pltpu.SemaphoreType.DMA((steps,)),
             pltpu.SemaphoreType.DMA((steps,)),
             pltpu.SemaphoreType.DMA((3,)),
+            pltpu.SemaphoreType.REGULAR((len(chain_of(n)), 2)),
         ],
         compiler_params=pltpu.CompilerParams(collective_id=0, has_side_effects=True, vmem_limit_bytes=60 * 2**20),
     )(x, b, projectors.transpose(1, 2, 3, 0), bits)

time: 136 us -> 127 us (0.934)
  Pallas kernels: 132 us -> 124 us
    pallas_call x1, Pallas kernels: 132 us -> 124 us  [shards(): pl.pallas_call(functools.partial(kernel, n), out_shape=jax.ShapeDtypeStru...]
where the time goes in v2:
time: 127 us; the launch traced here: 126 us
  Pallas kernels  124 us (98%)
  local copies, waits for them, and re-layouts  2.31 us (2%)
    pallas_call x1, Pallas kernels, shards(): pl.pallas_call(functools.partial(kernel, n), out_shape=jax.ShapeDtypeStru...  124 us

profile of v2, /device:TPU:37, one launch (start us, length us, event | category | flops | bytes accessed | tf_op | source)
XLA Modules:
  0.0 126.5 jit_solution(13084956870263791525)
XLA Ops:
  0.0 124.2 %shard_map.46 = f32[1,32,2,2,8,256]{5,4,3,2,1,0:T(8,128)} custom-call(bf16[256,1024]{1,0:T(8,128)(2,1)} %bitcast.12, bf16[8,2,2,512,128]{4,3,2,1,0:T(8,128)(2,1)} %bitcast.11, f32[2,2,2,8]{3,2,1,0:T(2,128)} %bitcast.13, s32[1,8]{1,0:T(1,128)} %bits_hbm.1), custom_call_target="tpu_custom_call" | custom-call | tf_op jit(solution)/shard_map/pallas_call | solution.py:229
  124.2 2.3 %copy.7 = f32[1,32,2,2,8,256]{5,4,3,2,1,0:T(8,128)} copy(f32[1,32,2,2,8,256]{5,4,3,2,1,0:T(8,128)} %shard_map.46) | data formatting | bytes 2097152

commit v3 on v2

--- a/solution.py
+++ b/solution.py
@@ -23,6 +23,7 @@
 
 
 NEAR = 3
+EARLY = 8
 
 
 def chain_of(n):
@@ -33,7 +34,7 @@
     return rounds
 
 
-def kernel(n, x_hbm, b_hbm, p_hbm, bits_hbm, out, parts, even_w, odd_w, rows_t, rows, send, last, p_s, bits_s,
+def kernel(n, x_hbm, b_hbm, p_hbm, bits_hbm, last, final_w, final_p, parts, even_w, odd_w, rows_t, rows, send, p_s, bits_s,
            send1, recv1, send2, recv2, bsend, brecv, bown, small, chain):
     z = lax.axis_index("wide")
     core = lax.axis_index("batch")
@@ -80,32 +81,36 @@
                 copy.start()
 
     rounds = chain_of(n)
+
+    def greet(k):
+        if k < len(rounds):
+            for way, to in enumerate((rounds[k], n - rounds[k])):
+                pl.semaphore_signal(chain.at[k, way], inc=1, device_id={"wide": lax.rem(z + to, n)}, device_id_type=MESH)
+
     reach = NEAR
-    start(1, reach)
+    greet(0)
+    start(1, min(reach, EARLY))
     for s in range(steps):
         push(s).start()
         pull(s).start()
-    near = 2 * NEAR
     for k, hop in enumerate(rounds):
-        pl.semaphore_signal(chain.at[k, 0], inc=1, device_id={"wide": lax.rem(z + hop, n)}, device_id_type=MESH)
-        pl.semaphore_signal(chain.at[k, 1], inc=1, device_id={"wide": lax.rem(z + n - hop, n)}, device_id_type=MESH)
-        pl.semaphore_wait(chain.at[k, 0], 1)
-        pl.semaphore_wait(chain.at[k, 1], 1)
-        if reach < near:
-            start(reach + 1, near)
+        for way in range(2):
+            pl.semaphore_wait(chain.at[k, way], 1)
+        greet(k + 1)
+        start(reach + 1, min(reach + hop, EARLY))
         reach += hop
 
     def rest(odd):
         for dests in (0, 1):
             for (d, _), copy in zip(hops, first):
-                if abs(d) > near and (d + odd + dests) % 2 == 0:
+                if abs(d) > EARLY and (d + odd + dests) % 2 == 0:
                     copy.start()
 
-    @pl.when(lax.rem(z, 2) == 0)
+    @pl.when(lax.rem(z + core, 2) == 0)
     def _():
         rest(0)
 
-    @pl.when(lax.rem(z, 2) == 1)
+    @pl.when(lax.rem(z + core, 2) == 1)
     def _():
         rest(1)
 
@@ -128,7 +133,7 @@
     def one_hot(shape, hit):
         return jnp.where(hit(lax.broadcasted_iota(jnp.int32, shape, 0), lax.broadcasted_iota(jnp.int32, shape, 1)), 1.0, 0.0).astype(BF16)
 
-    def prepare_even(i, s):
+    def prepare_even(into, s):
         perm = one_hot((2 * half, 2 * half), lambda j, r: r == (j % quarter) * 4 + j // quarter)
         for h in range(2):
             for uh in range(2):
@@ -140,7 +145,7 @@
                             re, im = got[k:k + quarter, :lanes], got[k:k + quarter, lanes:]
                             u = uh * half + ub * quarter
                             for p, q, what in ((0, 0, re), (0, 1, im), (1, 0, -im), (1, 1, re)):
-                                even_w[i, pl.ds((p * 2 + h) * group + u, quarter), pl.ds((q * 2 + g) * group + wt * lanes, lanes)] = what
+                                into[pl.ds((p * 2 + h) * group + u, quarter), pl.ds((q * 2 + g) * group + wt * lanes, lanes)] = what
 
     def prepare_odd(i, s):
         perm = one_hot((depth, depth), lambda r, j: r == (j % half) * 4 + j // half)
@@ -156,7 +161,7 @@
 
     def prepare(i, _):
         arrived(2 * i)
-        prepare_even(i, 2 * i)
+        prepare_even(even_w.at[i], 2 * i)
         arrived(2 * i + 1)
         prepare_odd(i, 2 * i + 1)
         return 0
@@ -168,10 +173,11 @@
     for copy in local:
         copy.wait()
 
+    def chosen(s, part, g):
+        return jnp.where(bits_s[0, s] == 1, p_s[1, part, g, s], p_s[0, part, g, s])
+
     def project(s, g, y_re, y_im):
-        one = bits_s[0, s] == 1
-        p_re = jnp.where(one, p_s[1, 0, g, s], p_s[0, 0, g, s])
-        p_im = jnp.where(one, p_s[1, 1, g, s], p_s[0, 1, g, s])
+        p_re, p_im = chosen(s, 0, g), chosen(s, 1, g)
         return p_re * y_re - p_im * y_im, p_re * y_im + p_im * y_re
 
     def at(q, g):
@@ -204,7 +210,10 @@
     own = pltpu.make_async_copy(block(send, z, None), block(last, z, None), small.at[0])
     own.start()
     arrived(7)
-    prepare_even(3, 7)
+    prepare_even(final_w, 7)
+    for part in range(2):
+        for g in range(2):
+            final_p[:, at(part, g)] = jnp.zeros((8, group), F32) + chosen(7, part, g)
     for s in range(steps):
         push(s).wait_send()
     for copy in first:
@@ -212,12 +221,26 @@
     own.wait()
     for copy in second:
         copy.wait_recv()
-    for g in range(2):
-        z_re, z_im = project(7, g, dot(last[...], even_w[3, :, at(0, g)]), dot(last[...], even_w[3, :, at(1, g)]))
-        out[0, :, 0, g] = z_re.reshape(n, wide, group)
-        out[0, :, 1, g] = z_im.reshape(n, wide, group)
     for copy in second:
         copy.wait_send()
+
+
+def final_kernel(last, weights, p, out, held, sems):
+    columns, _, _, wide, group = held.shape
+
+    def at(q, g):
+        return pl.ds((q * 2 + g) * group, group)
+
+    copies = []
+    for g in range(2):
+        y_re, y_im = dot(last[...], weights[:, at(0, g)]), dot(last[...], weights[:, at(1, g)])
+        p_re, p_im = p[0:1, at(0, g)], p[0:1, at(1, g)]
+        held[:, 0, g] = (p_re * y_re - p_im * y_im).reshape(columns, wide, group)
+        held[:, 1, g] = (p_re * y_im + p_im * y_re).reshape(columns, wide, group)
+        copies.append(pltpu.make_async_copy(held.at[:, :, g], out.at[0, :, :, g], sems.at[g]))
+        copies[-1].start()
+    for copy in copies:
+        copy.wait()
 
 
 def shards(n, initial, branches, projectors, bits):
@@ -226,18 +249,21 @@
     x = initial[0].transpose(0, 4, 1, 2, 3).reshape(columns * wide, 4 * group)
     b = branches.reshape(steps, 2, 2, half, 2, 2, group // 2).transpose(0, 1, 2, 3, 5, 4, 6).reshape(steps, 2, 2, half * 4, group // 2)
     hops = len(hops_of(n))
-    return pl.pallas_call(
+    last, weights, p = pl.pallas_call(
         functools.partial(kernel, n),
-        out_shape=jax.ShapeDtypeStruct((1, columns, 2, 2, wide, group), F32),
-        in_specs=[pl.BlockSpec(memory_space=pl.ANY)] * 4,
-        out_specs=pl.BlockSpec(memory_space=pltpu.VMEM),
+        out_shape=[
+            jax.ShapeDtypeStruct((group, 4 * group), BF16),
+            jax.ShapeDtypeStruct((4 * group, 4 * group), BF16),
+            jax.ShapeDtypeStruct((8, 4 * group), F32),
+        ],
+        in_specs=[pl.BlockSpec(memory_space=pltpu.HBM)] * 4,
+        out_specs=[pl.BlockSpec(memory_space=pltpu.VMEM)] * 3,
         scratch_shapes=[
             pltpu.VMEM((2, steps, 2, 2, half * 4, group // 2), BF16),
-            pltpu.VMEM((4, 4 * group, 4 * group), BF16),
+            pltpu.VMEM((3, 4 * group, 4 * group), BF16),
             pltpu.VMEM((4, 4 * group, 4 * group), BF16),
             pltpu.VMEM((group, 4 * group), BF16),
             pltpu.VMEM((4 * group, group), BF16),
-            pltpu.VMEM((group, 4 * group), BF16),
             pltpu.VMEM((group, 4 * group), BF16),
             pltpu.SMEM((2, 2, 2, steps), F32),
             pltpu.SMEM((1, steps), jnp.int32),
@@ -251,8 +277,16 @@
             pltpu.SemaphoreType.DMA((3,)),
             pltpu.SemaphoreType.REGULAR((len(chain_of(n)), 2)),
         ],
-        compiler_params=pltpu.CompilerParams(collective_id=0, has_side_effects=True, vmem_limit_bytes=60 * 2**20),
-    )(x, b, projectors.transpose(1, 2, 3, 0), bits)
+        compiler_params=pltpu.CompilerParams(collective_id=0, has_side_effects=True, vmem_limit_bytes=40 * 2**20),
+    )(*(pltpu.with_memory_space_constraint(a, pltpu.HBM) for a in (x, b, projectors.transpose(1, 2, 3, 0), bits)))
+    return pl.pallas_call(
+        final_kernel,
+        out_shape=jax.ShapeDtypeStruct((1, columns, 2, 2, wide, group), F32),
+        in_specs=[pl.BlockSpec(memory_space=pltpu.VMEM)] * 3,
+        out_specs=pl.BlockSpec(memory_space=pl.ANY),
+        scratch_shapes=[pltpu.VMEM((columns, 2, 2, wide, group), F32), pltpu.SemaphoreType.DMA((2,))],
+        compiler_params=pltpu.CompilerParams(vmem_limit_bytes=16 * 2**20),
+    )(last, weights, p)
 
 
 def solution(mesh):

time: 127 us -> 121 us (0.953)
  Pallas kernels: 124 us -> 121 us
  local copies, waits for them, and re-layouts: 2.31 us -> 0 us
    pallas_call x1 -> x2, Pallas kernels: 124 us -> 121 us  [the longest x1 120 us: shards(): pl.pallas_call(functools.partial(kernel, n), out_shape=[jax.ShapeDtypeStr...]
    unnamed x1 -> x0, local copies, waits for them, and re-layouts: 2.31 us -> none
where the time goes in v3:
time: 121 us
  Pallas kernels  121 us (100%)
    pallas_call x1, Pallas kernels, shards(): pl.pallas_call(functools.partial(kernel, n), out_shape=[jax.ShapeDtypeStr...  120 us

profile of v3, /device:TPU:37, one launch (start us, length us, event | category | flops | bytes accessed | tf_op | source)
XLA Modules:
  0.0 121.1 jit_solution(15482724860010569253)
XLA Ops:
  0.0 119.6 %shard_map.46 = (bf16[256,1024]{1,0:T(8,128)(2,1)S(1)}, bf16[1024,1024]{1,0:T(8,128)(2,1)S(1)}, f32[8,1024]{1,0:T(8,128)S(1)}) custom-call(bf16[256,1024]{1,0:T(8,128)(2,1)} %bitcast.12, bf16[8,2,2,512,128]{4,3,2,1,0:T(8,128)(2,1)} %bitcast.11, f32[2,2,2,8]{3,2,1,0:T(2,128)} %bitcast.13, s32[1,8]{1,0:T(1,128)} %bits_hbm.1), custom_call_target="tpu_custom_call" | custom-call | tf_op jit(solution)/shard_map/pallas_call | solution.py:252
  119.6 1.5 %shard_map.47 = f32[1,32,2,2,8,256]{5,4,3,2,1,0:T(8,128)} custom-call(bf16[256,1024]{1,0:T(8,128)(2,1)S(1)} %get-tuple-element.8.last, bf16[1024,1024]{1,0:T(8,128)(2,1)S(1)} %get-tuple-element.9.weights, f32[8,1024]{1,0:T(8,128)S(1)} %get-tuple-element.10.p), custom_call_target="tpu_custom_call" | custom-call | tf_op jit(solution)/shard_map/pallas_call | solution.py:282

commit v4 on v3

--- a/solution.py
+++ b/solution.py
@@ -76,7 +76,7 @@
     first = exchange(x_hbm, rows_t, send1, recv1)
 
     def start(nearest, farthest):
-        for (d, _), copy in reversed(list(zip(hops, first))):
+        for (d, _), copy in zip(hops, first):
             if nearest <= abs(d) <= farthest:
                 copy.start()
 

time: 121 us -> 121 us (level)
  no operation moved by 1% of the time
where the time goes in v4:
time: 121 us; the launch traced here: 120 us
  Pallas kernels  120 us (99%)
    pallas_call x1, Pallas kernels, shards(): pl.pallas_call(functools.partial(kernel, n), out_shape=[jax.ShapeDtypeStr...  119 us

profile of v4, /device:TPU:37, one launch (start us, length us, event | category | flops | bytes accessed | tf_op | source)
XLA Modules:
  0.0 120.5 jit_solution(9315775582447955702)
XLA Ops:
  0.0 118.9 %shard_map.46 = (bf16[256,1024]{1,0:T(8,128)(2,1)S(1)}, bf16[1024,1024]{1,0:T(8,128)(2,1)S(1)}, f32[8,1024]{1,0:T(8,128)S(1)}) custom-call(bf16[256,1024]{1,0:T(8,128)(2,1)} %bitcast.12, bf16[8,2,2,512,128]{4,3,2,1,0:T(8,128)(2,1)} %bitcast.11, f32[2,2,2,8]{3,2,1,0:T(2,128)} %bitcast.13, s32[1,8]{1,0:T(1,128)} %bits_hbm.1), custom_call_target="tpu_custom_call" | custom-call | tf_op jit(solution)/shard_map/pallas_call | solution.py:252
  118.9 1.5 %shard_map.47 = f32[1,32,2,2,8,256]{5,4,3,2,1,0:T(8,128)} custom-call(bf16[256,1024]{1,0:T(8,128)(2,1)S(1)} %get-tuple-element.8.last, bf16[1024,1024]{1,0:T(8,128)(2,1)S(1)} %get-tuple-element.9.weights, f32[8,1024]{1,0:T(8,128)S(1)} %get-tuple-element.10.p), custom_call_target="tpu_custom_call" | custom-call | tf_op jit(solution)/shard_map/pallas_call | solution.py:282

commit v5 on v4

--- a/solution.py
+++ b/solution.py
@@ -220,9 +220,8 @@
         copy.wait_send()
     own.wait()
     for copy in second:
+        copy.wait_send()
         copy.wait_recv()
-    for copy in second:
-        copy.wait_send()
 
 
 def final_kernel(last, weights, p, out, held, sems):
@@ -232,13 +231,16 @@
         return pl.ds((q * 2 + g) * group, group)
 
     copies = []
-    for g in range(2):
-        y_re, y_im = dot(last[...], weights[:, at(0, g)]), dot(last[...], weights[:, at(1, g)])
-        p_re, p_im = p[0:1, at(0, g)], p[0:1, at(1, g)]
-        held[:, 0, g] = (p_re * y_re - p_im * y_im).reshape(columns, wide, group)
-        held[:, 1, g] = (p_re * y_im + p_im * y_re).reshape(columns, wide, group)
-        copies.append(pltpu.make_async_copy(held.at[:, :, g], out.at[0, :, :, g], sems.at[g]))
-        copies[-1].start()
+    part = columns // 2
+    for top in (0, part):
+        for g in range(2):
+            some = last[pl.ds(top * wide, part * wide), :]
+            y_re, y_im = dot(some, weights[:, at(0, g)]), dot(some, weights[:, at(1, g)])
+            p_re, p_im = p[0:1, at(0, g)], p[0:1, at(1, g)]
+            held[pl.ds(top, part), 0, g] = (p_re * y_re - p_im * y_im).reshape(part, wide, group)
+            held[pl.ds(top, part), 1, g] = (p_re * y_im + p_im * y_re).reshape(part, wide, group)
+            copies.append(pltpu.make_async_copy(held.at[pl.ds(top, part), :, g], out.at[0, pl.ds(top, part), :, g], sems.at[len(copies)]))
+            copies[-1].start()
     for copy in copies:
         copy.wait()
 
@@ -284,7 +286,7 @@
         out_shape=jax.ShapeDtypeStruct((1, columns, 2, 2, wide, group), F32),
         in_specs=[pl.BlockSpec(memory_space=pltpu.VMEM)] * 3,
         out_specs=pl.BlockSpec(memory_space=pl.ANY),
-        scratch_shapes=[pltpu.VMEM((columns, 2, 2, wide, group), F32), pltpu.SemaphoreType.DMA((2,))],
+        scratch_shapes=[pltpu.VMEM((columns, 2, 2, wide, group), F32), pltpu.SemaphoreType.DMA((4,))],
         compiler_params=pltpu.CompilerParams(vmem_limit_bytes=16 * 2**20),
     )(last, weights, p)
 

time: 121 us -> 120 us (level)
  no operation moved by 1% of the time
where the time goes in v5:
time: 120 us
  Pallas kernels  120 us (100%)
    pallas_call x1, Pallas kernels, shards(): pl.pallas_call(functools.partial(kernel, n), out_shape=[jax.ShapeDtypeStr...  119 us

profile of v5, /device:TPU:37, one launch (start us, length us, event | category | flops | bytes accessed | tf_op | source)
XLA Modules:
  0.0 120.4 jit_solution(3582467135186196862)
XLA Ops:
  0.0 118.9 %shard_map.46 = (bf16[256,1024]{1,0:T(8,128)(2,1)S(1)}, bf16[1024,1024]{1,0:T(8,128)(2,1)S(1)}, f32[8,1024]{1,0:T(8,128)S(1)}) custom-call(bf16[256,1024]{1,0:T(8,128)(2,1)} %bitcast.12, bf16[8,2,2,512,128]{4,3,2,1,0:T(8,128)(2,1)} %bitcast.11, f32[2,2,2,8]{3,2,1,0:T(2,128)} %bitcast.13, s32[1,8]{1,0:T(1,128)} %bits_hbm.1), custom_call_target="tpu_custom_call" | custom-call | tf_op jit(solution)/shard_map/pallas_call | solution.py:254
  118.9 1.5 %shard_map.47 = f32[1,32,2,2,8,256]{5,4,3,2,1,0:T(8,128)} custom-call(bf16[256,1024]{1,0:T(8,128)(2,1)S(1)} %get-tuple-element.8.last, bf16[1024,1024]{1,0:T(8,128)(2,1)S(1)} %get-tuple-element.9.weights, f32[8,1024]{1,0:T(8,128)S(1)} %get-tuple-element.10.p), custom_call_target="tpu_custom_call" | custom-call | tf_op jit(solution)/shard_map/pallas_call | solution.py:284

commit v6 on v4

--- a/solution.py
+++ b/solution.py
@@ -90,15 +90,16 @@
     reach = NEAR
     greet(0)
     start(1, min(reach, EARLY))
-    for s in range(steps):
-        push(s).start()
-        pull(s).start()
     for k, hop in enumerate(rounds):
         for way in range(2):
             pl.semaphore_wait(chain.at[k, way], 1)
         greet(k + 1)
         start(reach + 1, min(reach + hop, EARLY))
         reach += hop
+
+    for s in range(steps):
+        push(s).start()
+        pull(s).start()
 
     def rest(odd):
         for dests in (0, 1):

time: 121 us -> 120 us (level)
  no operation moved by 1% of the time
where the time goes in v6:
time: 120 us
  Pallas kernels  120 us (100%)
    pallas_call x1, Pallas kernels, shards(): pl.pallas_call(functools.partial(kernel, n), out_shape=[jax.ShapeDtypeStr...  119 us

profile of v6, /device:TPU:37, one launch (start us, length us, event | category | flops | bytes accessed | tf_op | source)
XLA Modules:
  0.0 120.4 jit_solution(17102703007313328420)
XLA Ops:
  0.0 118.9 %shard_map.46 = (bf16[256,1024]{1,0:T(8,128)(2,1)S(1)}, bf16[1024,1024]{1,0:T(8,128)(2,1)S(1)}, f32[8,1024]{1,0:T(8,128)S(1)}) custom-call(bf16[256,1024]{1,0:T(8,128)(2,1)} %bitcast.12, bf16[8,2,2,512,128]{4,3,2,1,0:T(8,128)(2,1)} %bitcast.11, f32[2,2,2,8]{3,2,1,0:T(2,128)} %bitcast.13, s32[1,8]{1,0:T(1,128)} %bits_hbm.1), custom_call_target="tpu_custom_call" | custom-call | tf_op jit(solution)/shard_map/pallas_call | solution.py:253
  118.9 1.5 %shard_map.47 = f32[1,32,2,2,8,256]{5,4,3,2,1,0:T(8,128)} custom-call(bf16[256,1024]{1,0:T(8,128)(2,1)S(1)} %get-tuple-element.8.last, bf16[1024,1024]{1,0:T(8,128)(2,1)S(1)} %get-tuple-element.9.weights, f32[8,1024]{1,0:T(8,128)S(1)} %get-tuple-element.10.p), custom_call_target="tpu_custom_call" | custom-call | tf_op jit(solution)/shard_map/pallas_call | solution.py:283
